TPU v7x, 32 devices: a whole 2x2x4 slice. The times are simulated.
32 devices in a mesh: ctx: 8 (over z, y), kvh: 4 (over x, core).
Axes of the slice: x: 2, y: 2, z: 4, core: 2. Of those that a mesh axis runs over, the one named last changes fastest.
Arguments:
- queries: bfloat16 [2048, 2048], P(('ctx', 'kvh')), may hold values from -42 to 42
- keys: bfloat16 [2048, 512], P(('ctx', 'kvh')), may hold values from -6 to 6
- values: bfloat16 [2048, 512], P(('ctx', 'kvh')), may hold values from -6 to 6
- doc_lengths: int32 [16], replicated, may hold values from 1 to 1024, 2048 in all
Outputs:
- attended: bfloat16 [2048, 2048], P(('ctx', 'kvh'))
Inputs may be any that keep to these rules, and one draw needn't show every extreme that they name: `doc_lengths`: positive lengths that sum to 2048.
All inputs are finite; a program needn't handle non-finite values.
Results may differ from a plain program's by a relative error of at most 0.005.
Values may be sent and summed in bfloat16 or wider, within the bound.
A program may use at most 64 MiB of HBM per device.

v0:
```python
import jax
import jax.numpy as jnp
from jax import lax
from jax.sharding import PartitionSpec as P

HEAD_SIZE = 128
SINK = 128


def document_of(positions, starts):
    return jnp.sum((positions[:, None] >= starts[None, :]).astype(jnp.int32), axis=1)


def absorb_block(state, q_half, allowed, k_block, v_block, kv_heads):
    running_max, running_sum, accum = state
    count = k_block.shape[0]
    k_heads = k_block.reshape(count, kv_heads, HEAD_SIZE)
    v_heads = v_block.reshape(count, kv_heads, HEAD_SIZE)
    scores = jnp.einsum(
        "qgrd,kgd->grqk", q_half, k_heads, preferred_element_type=jnp.float32
    ) * HEAD_SIZE ** (-0.5)
    scores = jnp.where(allowed[None, None], scores, jnp.float32(-1e30))
    new_max = jnp.maximum(running_max, jnp.max(scores, axis=-1))
    correction = jnp.exp(running_max - new_max)
    expo = jnp.where(allowed[None, None], jnp.exp(scores - new_max[..., None]), jnp.float32(0.0))
    new_sum = running_sum * correction + jnp.sum(expo, axis=-1)
    product = jnp.einsum(
        "grqk,kgd->grqd", expo.astype(jnp.bfloat16), v_heads, preferred_element_type=jnp.float32
    )
    return (new_max, new_sum, accum * correction[..., None] + product)


def shards(queries, keys, values, doc_lengths):
    local_q, local_k, local_v = (
        lax.all_to_all(queries, "kvh", split_axis=1, concat_axis=0, tiled=True),
        lax.all_to_all(keys, "kvh", split_axis=1, concat_axis=0, tiled=True),
        lax.all_to_all(values, "kvh", split_axis=1, concat_axis=0, tiled=True),
    )
    tok = local_q.shape[0]
    half = tok // 2
    place = lax.axis_index("ctx")
    kv_heads = local_k.shape[1] // HEAD_SIZE
    query_group = local_q.shape[1] // local_k.shape[1]
    starts = jnp.cumsum(doc_lengths) - doc_lengths
    offsets = jnp.arange(half, dtype=jnp.int32)
    lower_pos = place * tok + offsets
    upper_q = local_q[half:]
    upper_pos = place * tok + half + offsets
    segments = []
    for rows, positions in ((local_q[:half], lower_pos), (upper_q, upper_pos)):
        segments.append(
            (
                rows.reshape(half, kv_heads, query_group, HEAD_SIZE),
                positions,
                document_of(positions, starts),
            )
        )

    def absorb_all(states, k_block, v_block, k_pos):
        k_doc = document_of(k_pos, starts)
        updated = []
        for (q_half, q_pos, q_doc), state in zip(segments, states):
            causal = k_pos[None, :] <= q_pos[:, None]
            same_doc = q_doc[:, None] == k_doc[None, :]
            allowed = causal & (same_doc | (k_pos[None, :] < SINK))
            state = absorb_block(state, q_half, allowed, k_block, v_block, kv_heads)
            updated.append(state)
        return tuple(updated)

    empty = (
        jnp.full((kv_heads, query_group, half), -1e30, jnp.float32),
        jnp.zeros((kv_heads, query_group, half), jnp.float32),
        jnp.zeros((kv_heads, query_group, half, HEAD_SIZE), jnp.float32),
    )
    states = (empty, empty)
    carry = states
    k_piece = lax.all_gather(local_k, "ctx", axis=0, tiled=True)
    v_piece = lax.all_gather(local_v, "ctx", axis=0, tiled=True)
    count = k_piece.shape[0]
    block = 512

    def inner(state, number):
        first = number * block
        k_block = lax.dynamic_slice_in_dim(k_piece, first, block, 0)
        v_block = lax.dynamic_slice_in_dim(v_piece, first, block, 0)
        k_pos = first + jnp.arange(block, dtype=jnp.int32)
        return (absorb_all(state, k_block, v_block, k_pos), None)

    carry, unused = lax.scan(inner, carry, jnp.arange(count // block, dtype=jnp.int32))
    states = carry
    outputs = []
    for running_max, running_sum, accum in states:
        normed = accum / running_sum[..., None]
        outputs.append(
            jnp.transpose(normed, (2, 0, 1, 3))
            .reshape(half, kv_heads * query_group * HEAD_SIZE)
            .astype(jnp.bfloat16)
        )
    lower_out, upper_out = outputs
    merged = jnp.concatenate([lower_out, upper_out], axis=0)
    return lax.all_to_all(merged, "kvh", split_axis=0, concat_axis=1, tiled=True)


def solution(mesh):
    placed = (P(("ctx", "kvh"), None), P(("ctx", "kvh"), None), P(("ctx", "kvh"), None), P())
    return jax.shard_map(
        shards, mesh=mesh, in_specs=placed, out_specs=P(("ctx", "kvh"), None), check_vma=False
    )
```

profile of v0, /device:TPU:0, one launch (start us, length us, event | category | flops | bytes accessed | tf_op | source)
XLA Modules:
  0.0 105.5 jit_solution(18280515149646120339)
XLA Ops:
  0.0 0.8 copy-done
  0.8 0.6 copy_bitcast_fusion.1
  1.5 4.2 %all-to-all-start.2 = ((bf16[64,4,128]{2,0,1:T(8,128)(2,1)}), bf16[64,4,128]{2,0,1:T(8,128)(2,1)S(1)}, u32[]{:S(2)}, u32[]{:S(2)}) async-start(bf16[64,4,128]{2,0,1:T(8,128)(2,1)} %copy_bitcast_fusion.1), calls=%async_computation.2 | async-start | bytes 131072 | tf_op jit(solution)/shard_map/all_to_all | solution.py:37
  5.7 0.7 copy.35
  6.6 0.7 sub.29
  7.3 0.6 copy_bitcast_fusion.2
  8.0 0.7 copy.54
  8.8 1.1 %all-to-all-done.2 = bf16[64,4,128]{2,0,1:T(8,128)(2,1)S(1)} async-done(((bf16[64,4,128]{2,0,1:T(8,128)(2,1)}), bf16[64,4,128]{2,0,1:T(8,128)(2,1)S(1)}, u32[]{:S(2)}, u32[]{:S(2)}) %all-to-all-start.2) | async-done | bytes 65568 | tf_op jit(solution)/shard_map/all_to_all | solution.py:37
  9.8 3.3 %all-to-all-start = ((bf16[64,4,128]{2,0,1:T(8,128)(2,1)}), bf16[64,4,128]{2,0,1:T(8,128)(2,1)S(1)}, u32[]{:S(2)}, u32[]{:S(2)}) async-start(bf16[64,4,128]{2,0,1:T(8,128)(2,1)} %copy_bitcast_fusion.2), calls=%async_computation | async-start | bytes 131072 | tf_op jit(solution)/shard_map/all_to_all | solution.py:36
  13.1 32.4 %all_gather.7 = bf16[2048,128]{1,0:T(8,128)(2,1)S(1)} all-gather(bf16[256,128]{1,0:T(8,128)(2,1)S(1)} %bitcast.142), channel_id=1, replica_groups=mesh['ctx'=8,'kvh'=4] {'ctx'}, dimensions={0}, use_global_device_ids=true | all-gather | bytes 589824 | tf_op jit(solution)/shard_map/all_gather | solution.py:78
  45.5 3.4 %all-to-all-start.1 = ((bf16[64,4,512]{2,0,1:T(8,128)(2,1)}), bf16[64,4,512]{2,0,1:T(8,128)(2,1)S(1)}, u32[]{:S(2)}, u32[]{:S(2)}) async-start(bf16[64,4,512]{2,0,1:T(8,128)(2,1)} %bitcast.100), calls=%async_computation.1 | async-start | bytes 524288 | tf_op jit(solution)/shard_map/all_to_all | solution.py:35
  48.9 31.5 %all_gather.6 = bf16[2048,128]{1,0:T(8,128)(2,1)S(1)} all-gather(bf16[256,128]{1,0:T(8,128)(2,1)S(1)} %bitcast.143), channel_id=1, replica_groups=mesh['ctx'=8,'kvh'=4] {'ctx'}, dimensions={0}, use_global_device_ids=true | all-gather | bytes 589824 | tf_op jit(solution)/shard_map/all_gather | solution.py:77
  80.5 14.9 %while.21 = (s32[]{:T(128)}, f32[1,4,128]{2,1,0:T(4,128)S(1)}, f32[1,4,128]{2,1,0:T(4,128)S(1)}, f32[1,4,128,128]{3,2,1,0:T(8,128)S(1)}, f32[1,4,128]{2,1,0:T(4,...) while((s32[]{:T(128)}, f32[1,4,128]{2,1,0:T(4,128)S(1)}, ...), condition=%wide.region_9.10_spmd.clone, body=%wide.region_3.9_spmd.clone.sunk | while | flops 274103552 | bytes 8730989 | solution.py:89
  80.6 0.6 dynamic_slice.42
  82.2 0.3 fusion.63
  82.8 0.4 fusion.69
  83.2 0.3 fusion.65
  83.8 0.4 fusion.70
  84.3 0.6 dynamic_slice.42
  86.5 0.4 fusion.69
  86.9 0.3 fusion.65
  87.5 0.4 fusion.70
  88.0 0.6 dynamic_slice.42
  90.2 0.4 fusion.69
  90.6 0.3 fusion.65
  91.2 0.4 fusion.70
  91.7 0.6 dynamic_slice.42
  93.9 0.4 fusion.69
  94.4 0.3 fusion.65
  94.9 0.4 fusion.70
  95.9 8.9 %all_to_all.73 = bf16[4,64,512]{2,1,0:T(8,128)(2,1)S(1)} all-to-all(bf16[4,64,512]{2,1,0:T(8,128)(2,1)S(1)} %bitcast.138), channel_id=1, replica_groups=mesh['ctx'=8,'kvh'=4] {'kvh'}, dimensions={0} | all-to-all | bytes 524288 | tf_op jit(solution)/shard_map/all_to_all | solution.py:101
  104.8 0.7 copy.50
  (84 shorter events, 5.2 us)
Async XLA Ops:
  0.0 0.8 copy-start
  0.0 7.3 %copy-start.2 = (bf16[64,512]{1,0:T(8,128)(2,1)S(1)}, bf16[64,512]{1,0:T(8,128)(2,1)}, u32[]{:S(2)}) copy-start(bf16[64,512]{1,0:T(8,128)(2,1)} %param.7) | copy-start | bytes 196612
  0.8 7.2 %copy-start.1 = (bf16[64,2048]{1,0:T(8,128)(2,1)S(1)}, bf16[64,2048]{1,0:T(8,128)(2,1)}, u32[]{:S(2)}) copy-start(bf16[64,2048]{1,0:T(8,128)(2,1)} %param.6) | copy-start | bytes 786436
  1.5 8.4 %all-to-all-start.2 = ((bf16[64,4,128]{2,0,1:T(8,128)(2,1)}), bf16[64,4,128]{2,0,1:T(8,128)(2,1)S(1)}, u32[]{:S(2)}, u32[]{:S(2)}) async-start(bf16[64,4,128]{2,0,1:T(8,128)(2,1)} %copy_bitcast_fusion.1), calls=%async_computation.2 | async-start | bytes 131072 | tf_op jit(solution)/shard_map/all_to_all | solution.py:37
  9.8 35.7 %all-to-all-start = ((bf16[64,4,128]{2,0,1:T(8,128)(2,1)}), bf16[64,4,128]{2,0,1:T(8,128)(2,1)S(1)}, u32[]{:S(2)}, u32[]{:S(2)}) async-start(bf16[64,4,128]{2,0,1:T(8,128)(2,1)} %copy_bitcast_fusion.2), calls=%async_computation | async-start | bytes 131072 | tf_op jit(solution)/shard_map/all_to_all | solution.py:36
  45.5 34.9 %all-to-all-start.1 = ((bf16[64,4,512]{2,0,1:T(8,128)(2,1)}), bf16[64,4,512]{2,0,1:T(8,128)(2,1)S(1)}, u32[]{:S(2)}, u32[]{:S(2)}) async-start(bf16[64,4,512]{2,0,1:T(8,128)(2,1)} %bitcast.100), calls=%async_computation.1 | async-start | bytes 524288 | tf_op jit(solution)/shard_map/all_to_all | solution.py:35
where the time goes:
time: 106 us
  blocking collectives  72.7 us (69%)
  starting transfers between devices  10.9 us (10%)
  local copies, waits for them, and re-layouts  7.19 us (7%)
  matrix products  6.06 us (6%)
  other arithmetic  4.35 us (4%)
  loops' own time  3.07 us (3%)
  waiting for transfers between devices  1.08 us (1%)
    all_gather x1, blocking collectives, shards(): v_piece = lax.all_gather(local_v, 'ctx', axis=0, tiled=True)  32.4 us
    all_gather x1, blocking collectives, shards(): k_piece = lax.all_gather(local_k, 'ctx', axis=0, tiled=True)  31.5 us
    all_to_all x1, blocking collectives, shards(): lax.all_to_all(merged, 'kvh', split_axis=0, concat_axis=1, tiled=True)  8.88 us
    all_to_all x1, starting transfers between devices, shards(): lax.all_to_all(values, 'kvh', split_axis=1, concat_axis=0, tiled=True)  4.24 us
    dot_general x8, matrix products, absorb_block(): jnp.einsum('grqk,kgd->grqd', expo.astype(jnp.bfloat16), v_heads, preferre...  3.57 us
    all_to_all x1, starting transfers between devices, shards(): lax.all_to_all(queries, 'kvh', split_axis=1, concat_axis=0, tiled=True)  3.41 us
    all_to_all x1, starting transfers between devices, shards(): lax.all_to_all(keys, 'kvh', split_axis=1, concat_axis=0, tiled=True)  3.28 us
    another operation x1, loops' own time, shards(): lax.scan(inner, carry, jnp.arange(count // block, dtype=jnp.int32))  3.07 us
  transfers between devices with their start and end apart: 3, of which 1 were waited for; matrix products, arithmetic and copies ran while one was open for 3% of the time, Pallas kernels for 0%

commit v1 on v0

v1 whole, which is shorter than its diff:
```python
import functools
import math

import jax
import jax.numpy as jnp
from jax import lax
from jax.experimental import pallas as pl
from jax.experimental.pallas import tpu as pltpu
from jax.sharding import PartitionSpec as P

HEAD_SIZE = 128
SINK = 128
NEG = -1e30


def attention_kernel(
    planes, reach, kv_heads, group,
    lens_ref, q_hbm, k_hbm, v_hbm, o_ref,
    kbuf, vbuf, qbuf, scores, bias,
    local_sem, send_sem, recv_sem, pair_send, pair_recv, sink_send,
):
    rows = k_hbm.shape[0]
    chip = 2 * rows
    plane = 4 * chip
    ctx, kvh = lax.axis_index("ctx"), lax.axis_index("kvh")
    z, y = ctx // 2, ctx % 2
    x, core = kvh // 2, kvh % 2
    col = 2 * y + x
    xcol, ycol, dcol = 2 * y + 1 - x, 2 * (1 - y) + x, 3 - col
    even = x == y
    bufs = (kbuf, vbuf)

    def dev(xx, yy, zz, cc):
        return (2 * zz + yy, 2 * xx + cc)

    to_x, to_y, partner = dev(1 - x, y, z, core), dev(x, 1 - y, z, core), dev(x, y, z, 1 - core)
    to_z = dev(x, y, z + 1, core)

    names = ["own", "S"] + [("Z", d) for d in range(1, reach + 1)]
    names += [("F", d, w) for d in range(1, reach) for w in "XYD"] + [("M", w) for w in "XYD"]
    index = {name: n for n, name in enumerate(names)}

    def at(slot, column, cc=None):
        return slot * plane + column * chip + (core if cc is None else cc) * rows

    def extra(which, cc=None):
        return reach * plane + which * chip + (core if cc is None else cc) * rows

    def view(t, start):
        return bufs[t].at[pl.ds(pl.multiple_of(start, rows), rows), :]

    finals = []

    def send(t, name, src, dst, device, cond):
        n = index[name]

        def make():
            return pltpu.make_async_remote_copy(
                src_ref=view(t, src), dst_ref=view(t, dst),
                send_sem=send_sem.at[t, n], recv_sem=recv_sem.at[t, n],
                device_id=device, device_id_type=pl.DeviceIdType.MESH,
            )

        @pl.when(cond)
        def _():
            make().start()

        finals.append((cond, make))

    def pair_copy(t, name, start, sem_only=False):
        n = index[name]
        return pltpu.make_async_remote_copy(
            src_ref=view(t, start), dst_ref=view(t, start),
            send_sem=pair_send.at[t, n], recv_sem=pair_recv.at[t, n],
            device_id=partner, device_id_type=pl.DeviceIdType.MESH,
        )

    pair_waits = ([], [])

    def arrive(t, name, start, other, cond):
        n = index[name]

        @pl.when(cond)
        def _():
            pltpu.make_async_remote_copy(
                src_ref=view(t, start), dst_ref=view(t, start),
                send_sem=send_sem.at[t, n], recv_sem=recv_sem.at[t, n],
                device_id=partner, device_id_type=pl.DeviceIdType.MESH,
            ).wait_recv()
            pair_copy(t, name, start).start()

        finals.append((cond, lambda: pair_copy(t, name, start)))
        pair_waits[t].append((cond, name, other))

    def both(start_of):
        return start_of(core), start_of(1 - core)

    def send_sinks(t, cond):
        for number in range(reach, planes):
            def make(number=number):
                return pltpu.make_async_remote_copy(
                    src_ref=view(t, at(0, 0)), dst_ref=view(t, extra(1)),
                    send_sem=sink_send.at[t, number], recv_sem=recv_sem.at[t, index["S"]],
                    device_id=dev(x, y, number, core), device_id_type=pl.DeviceIdType.MESH,
                )

            @pl.when(cond)
            def _():
                make().start()

            finals.append((cond, make))

    true = z >= 0

    def own(t):
        pltpu.make_async_copy((k_hbm, v_hbm)[t], view(t, at(0, col)), local_sem.at[t]).wait()
        send(t, ("Z", 1), at(0, col), at(1, col) if reach > 1 else extra(0), to_z, z + 1 < planes)
        send(t, ("M", "X"), at(0, col), at(0, col), to_x, xcol > col)
        send(t, ("M", "Y"), at(0, col), at(0, col), to_y, ycol > col)
        pair_copy(t, "own", at(0, col)).start()
        finals.append((true, lambda: pair_copy(t, "own", at(0, col))))
        pair_waits[t].append((true, "own", at(0, col, 1 - core)))
        send_sinks(t, (z == 0) & (col == 0))

    def column(t, d):
        start_of = (lambda cc: at(d, col, cc)) if d < reach else (lambda cc: extra(0, cc))
        here, other = both(start_of)
        arrive(t, ("Z", d), here, other, z >= d)
        if d < reach:
            send(t, ("Z", d + 1), here, at(d + 1, col) if d + 1 < reach else extra(0), to_z,
                 (z >= d) & (z + 1 < planes))
            send(t, ("F", d, "X"), here, here, to_x, z >= d)
            send(t, ("F", d, "Y"), here, here, to_y, z >= d)
        else:
            send(t, ("M", "X"), here, at(0, col), to_x, (z >= d) & (xcol < col))
            send(t, ("M", "Y"), here, at(0, col), to_y, (z >= d) & (ycol < col))

    def relay_m(t, cond):
        source = jnp.where(even, ycol, xcol)
        device = dev(jnp.where(even, 1 - x, x), jnp.where(even, y, 1 - y), z, core)
        send(t, ("M", "D"), at(0, source), at(0, source), device, cond(source, 3 - source))

    def mixed_early(t):
        for w, j in (("X", xcol), ("Y", ycol)):
            arrive(t, ("M", w), *both(lambda cc, j=j: at(0, j, cc)), j < col)
        relay_m(t, lambda s, d: s < d)
        send_sinks(t, (z == 0) & ((col == 1) | (col == 2)))

    def mixed_late(t):
        for w, j in (("X", xcol), ("Y", ycol)):
            arrive(t, ("M", w), *both(lambda cc, j=j: at(0, j, cc)), (j > col) & (z >= reach))
        relay_m(t, lambda s, d: (s > d) & (z >= reach))

    def mixed_diag(t, late):
        cond = ((dcol > col) & (z >= reach)) if late else (dcol < col)
        arrive(t, ("M", "D"), *both(lambda cc: at(0, dcol, cc)), cond)
        if not late:
            send_sinks(t, (z == 0) & (col == 3))

    def full(t, d):
        for w, j in (("X", xcol), ("Y", ycol)):
            arrive(t, ("F", d, w), *both(lambda cc, j=j: at(d, j, cc)), z >= d)
        source = jnp.where(even, xcol, ycol)
        device = dev(jnp.where(even, x, 1 - x), jnp.where(even, 1 - y, y), z, core)
        send(t, ("F", d, "D"), at(d, source), at(d, source), device, z >= d)

    def full_diag(t, d):
        arrive(t, ("F", d, "D"), *both(lambda cc: at(d, dcol, cc)), z >= d)

    def sink(t):
        arrive(t, "S", *both(lambda cc: extra(1, cc)), z >= reach)

    def from_pair(t):
        for cond, name, other in pair_waits[t]:
            @pl.when(cond)
            def _():
                pair_copy(t, name, other).wait_recv()

    pltpu.make_async_copy(k_hbm, view(0, at(0, col)), local_sem.at[0]).start()
    pltpu.make_async_copy(v_hbm, view(1, at(0, col)), local_sem.at[1]).start()
    q_copy = pltpu.make_async_copy(q_hbm, qbuf, local_sem.at[2])
    q_copy.start()
    barrier = pltpu.get_barrier_semaphore()
    for device in (to_x, to_y, partner):
        pl.semaphore_signal(barrier, inc=1, device_id=device, device_id_type=pl.DeviceIdType.MESH)
    for step in range(1, planes):
        pl.semaphore_signal(
            barrier, inc=1, device_id=dev(x, y, (z + step) % planes, core),
            device_id_type=pl.DeviceIdType.MESH,
        )
    pl.semaphore_wait(barrier, planes + 2)

    own(0)
    own(1)

    def clear(start, count, cond):
        @pl.when(cond)
        def _():
            for buf in bufs:
                buf[start:start + count, :] = jnp.zeros((count, buf.shape[1]), buf.dtype)

    for d in range(1, reach):
        clear(d * plane, plane, z < d)
    for j in range(1, 4):
        clear(j * chip, chip, (j > col) & (z < reach))
    clear(reach * plane, 2 * chip, z < reach)

    q_pos = ctx * (4 * rows) + kvh * rows + lax.broadcasted_iota(jnp.int32, (rows, 1), 0)
    first = jnp.zeros((rows, 1), jnp.int32)
    begin = jnp.int32(0)
    for n in range(lens_ref.shape[0]):
        first = jnp.where(q_pos >= begin, begin, first)
        begin = begin + lens_ref[n]
    lane = lax.broadcasted_iota(jnp.int32, (1, chip), 1)

    def set_bias(start, base):
        k_pos = base + lane
        sees = (k_pos <= q_pos) & ((k_pos >= first) | ((k_pos < SINK) & (k_pos >= 0)))
        bias[:, start:start + chip] = jnp.where(sees, jnp.float32(0.0), jnp.float32(NEG))

    nowhere = -planes * plane * 2
    for j in range(4):
        set_bias(j * chip, jnp.where(j <= col, z, z - reach) * plane + j * chip)
        for d in range(1, reach):
            set_bias(d * plane + j * chip, (z - d) * plane + j * chip)
    set_bias(reach * plane, (z - reach) * plane + col * chip)
    set_bias(reach * plane + chip, jnp.where((z > reach) | ((z == reach) & (col > 0)), 0, nowhere))

    def arrivals(t, part):
        if part == 0:
            column(t, 1)
            mixed_early(t)
        elif part == 1:
            for d in range(2, reach + 1):
                column(t, d)
            for d in range(1, reach):
                full(t, d)
            mixed_diag(t, False)
        else:
            mixed_late(t)

    def last(t):
        for d in range(1, reach):
            full_diag(t, d)
        sink(t)
        mixed_diag(t, True)

    for part in range(3):
        for t in range(2):
            arrivals(t, part)
    last(0)
    from_pair(0)
    q_copy.wait()

    keys = bias.shape[1]
    step = 2 * chip
    tall = group * rows
    size = HEAD_SIZE

    def head_q(h):
        return jnp.concatenate(
            [qbuf[:, (h * group + g) * size:(h * group + g + 1) * size] for g in range(group)], axis=0
        )

    def fold(op, value, total):
        for n in range(value.shape[1] // size):
            total = op(total, value[:, n * size:(n + 1) * size])
        return total

    def each(body, init):
        count = keys // step
        if count <= 8:
            for n in range(count):
                init = body(n, init)
            return init
        return lax.fori_loop(0, count, body, init)

    def cut(n):
        return pl.ds(n * step if isinstance(n, int) else pl.multiple_of(n * step, step), step)

    tops = []
    for h in range(kv_heads):
        qh = head_q(h)

        def score(n, top, h=h, qh=qh):
            s = lax.dot_general(
                qh, kbuf[cut(n), h * size:(h + 1) * size], (((1,), (1,)), ((), ())),
                preferred_element_type=jnp.float32,
            )
            s = s + jnp.concatenate([bias[:, cut(n)]] * group, axis=0)
            scores[h * tall:(h + 1) * tall, cut(n)] = s
            return fold(jnp.maximum, s, top)

        top = each(score, jnp.full((tall, size), NEG, jnp.float32))
        tops.append(jnp.max(top, axis=1, keepdims=True))

    last(1)
    from_pair(1)

    factor = jnp.float32(HEAD_SIZE ** -0.5 * math.log2(math.e))
    for h in range(kv_heads):
        def weigh(n, carry, h=h):
            total, acc = carry
            p = jnp.exp2((scores[h * tall:(h + 1) * tall, cut(n)] - tops[h]) * factor)
            acc = acc + jnp.dot(
                p.astype(jnp.bfloat16), vbuf[cut(n), h * size:(h + 1) * size],
                preferred_element_type=jnp.float32,
            )
            return fold(jnp.add, p, total), acc

        zero = jnp.zeros((tall, size), jnp.float32)
        total, acc = each(weigh, (zero, zero))
        out = (acc / jnp.sum(total, axis=1, keepdims=True)).astype(o_ref.dtype)
        for g in range(group):
            o_ref[:, (h * group + g) * size:(h * group + g + 1) * size] = out[g * rows:(g + 1) * rows]

    for cond, make in finals:
        @pl.when(cond)
        def _():
            make().wait_send()


def solution(mesh):
    planes = mesh.shape["ctx"] // 2
    reach = planes // 2

    def shards(queries, keys, values, doc_lengths):
        rows, width = keys.shape
        kv_heads = width // HEAD_SIZE
        group = queries.shape[1] // width
        span = (4 * reach + 2) * 2 * rows
        pieces = 2 + reach + 3 * (reach - 1) + 3
        return pl.pallas_call(
            functools.partial(attention_kernel, planes, reach, kv_heads, group),
            out_shape=jax.ShapeDtypeStruct(queries.shape, queries.dtype),
            in_specs=[pl.BlockSpec(memory_space=pltpu.SMEM)] + [pl.BlockSpec(memory_space=pl.ANY)] * 3,
            out_specs=pl.BlockSpec(memory_space=pltpu.VMEM),
            scratch_shapes=[
                pltpu.VMEM((span, width), keys.dtype),
                pltpu.VMEM((span, width), values.dtype),
                pltpu.VMEM(queries.shape, queries.dtype),
                pltpu.VMEM((kv_heads * group * rows, span), jnp.float32),
                pltpu.VMEM((rows, span), jnp.float32),
                pltpu.SemaphoreType.DMA((3,)),
                pltpu.SemaphoreType.DMA((2, pieces)),
                pltpu.SemaphoreType.DMA((2, pieces)),
                pltpu.SemaphoreType.DMA((2, pieces)),
                pltpu.SemaphoreType.DMA((2, pieces)),
                pltpu.SemaphoreType.DMA((2, planes)),
            ],
            compiler_params=pltpu.CompilerParams(
                collective_id=0, has_side_effects=True, vmem_limit_bytes=64 * 1024 * 1024 - 65536,
            ),
            name="attend",
        )(doc_lengths, queries, keys, values)

    placed = (P(("ctx", "kvh"), None), P(("ctx", "kvh"), None), P(("ctx", "kvh"), None), P())
    return jax.shard_map(
        shards, mesh=mesh, in_specs=placed, out_specs=P(("ctx", "kvh"), None), check_vma=False
    )
```

time: 106 us -> 30.8 us (0.29)
  the two profiles are of different devices: /device:TPU:0 before, /device:TPU:16 now
where the time goes in v1:
time: 30.8 us; the launch traced here: 30.6 us
  Pallas kernels  28.9 us (94%)
  local copies, waits for them, and re-layouts  1.67 us (5%)
    pallas_call x1, Pallas kernels, shards(): pl.pallas_call(functools.partial(attention_kernel, planes, reach, kv_head...  28.9 us
    unnamed x1, local copies, waits for them, and re-layouts  1.67 us

profile of v1, /device:TPU:16, one launch (start us, length us, event | category | flops | bytes accessed | tf_op | source)
XLA Modules:
  0.0 30.6 jit_solution(6669159346739153313)
XLA Ops:
  0.0 28.9 %attend.1 = bf16[64,2048]{1,0:T(8,128)(2,1)} custom-call(s32[16]{0:T(128)} %lens_ref.1, bf16[64,2048]{1,0:T(8,128)(2,1)} %q_hbm.1, bf16[64,512]{1,0:T(8,128)(2,1)} %k_hbm.1, bf16[64,512]{1,0:T(8,128)(2,1)} %v_hbm.1), custom_call_target="tpu_custom_call" | custom-call | tf_op jit(solution)/shard_map/attend/pallas_call | solution.py:333
  28.9 1.7 %copy.6 = bf16[64,2048]{1,0:T(8,128)(2,1)} copy(bf16[64,2048]{1,0:T(8,128)(2,1)} %attend.1) | data formatting | bytes 524288

commit v2 on v1

v2 whole, which is shorter than its diff:
```python
import functools
import math

import jax
import jax.numpy as jnp
from jax import lax
from jax.experimental import pallas as pl
from jax.experimental.pallas import tpu as pltpu
from jax.sharding import PartitionSpec as P

HEAD_SIZE = 128
SINK = 128
NEG = -1e30
CHUNKS = 1


def attention_kernel(
    planes, reach, kv_heads, group,
    lens_hbm, q_hbm, k_hbm, v_hbm, o_ref,
    lens_ref, kbuf, vbuf, qbuf, scores, bias,
    local_sem, send_sem, recv_sem, pair_send, pair_recv, far_send,
):
    rows = k_hbm.shape[0]
    chip = 2 * rows
    plane = 4 * chip
    ctx, kvh = lax.axis_index("ctx"), lax.axis_index("kvh")
    z, y = ctx // 2, ctx % 2
    x, core = kvh // 2, kvh % 2
    col = 2 * y + x
    xcol, ycol, dcol = 2 * y + 1 - x, 2 * (1 - y) + x, 3 - col
    bufs = (kbuf, vbuf)

    def dev(xx, yy, zz, cc):
        return (2 * zz + yy, 2 * xx + cc)

    to_x, to_y, partner = dev(1 - x, y, z, core), dev(x, 1 - y, z, core), dev(x, y, z, 1 - core)
    to_d = dev(1 - x, 1 - y, z, core)
    ways = (("X", to_x, xcol), ("Y", to_y, ycol), ("D", to_d, dcol))

    names = ["own", "S"] + [("Z", d) for d in range(1, reach + 1)]
    names += [("F", d, w) for d in range(1, reach) for w in "XYD"] + [("M", w) for w in "XYD"]
    index = {name: n for n, name in enumerate(names)}

    def at(slot, column, cc=None):
        return slot * plane + column * chip + (core if cc is None else cc) * rows

    def extra(which, cc=None):
        return reach * plane + which * chip + (core if cc is None else cc) * rows

    part = rows // CHUNKS

    def view(t, start):
        first = start + (t % CHUNKS) * part
        return bufs[t // CHUNKS].at[pl.ds(pl.multiple_of(first, part), part), :]

    finals = []

    def send(t, name, src, dst, device, cond, w=None):
        n = index[name]
        out = n if w is None else len(names) + "XYD".index(w)

        def make():
            return pltpu.make_async_remote_copy(
                src_ref=view(t, src), dst_ref=view(t, dst),
                send_sem=send_sem.at[t, out], recv_sem=recv_sem.at[t, n],
                device_id=device, device_id_type=pl.DeviceIdType.MESH,
            )

        @pl.when(cond)
        def _():
            make().start()

        finals.append((cond, make))

    def pair_copy(t, name, start, sem_only=False):
        n = index[name]
        return pltpu.make_async_remote_copy(
            src_ref=view(t, start), dst_ref=view(t, start),
            send_sem=pair_send.at[t, n], recv_sem=pair_recv.at[t, n],
            device_id=partner, device_id_type=pl.DeviceIdType.MESH,
        )

    pair_waits = [[] for _ in range(2 * CHUNKS)]

    def arrive(t, name, start, other, cond):
        n = index[name]

        @pl.when(cond)
        def _():
            pltpu.make_async_remote_copy(
                src_ref=view(t, start), dst_ref=view(t, start),
                send_sem=send_sem.at[t, n], recv_sem=recv_sem.at[t, n],
                device_id=partner, device_id_type=pl.DeviceIdType.MESH,
            ).wait_recv()
            pair_copy(t, name, start).start()

        finals.append((cond, lambda: pair_copy(t, name, start)))
        pair_waits[t].append((cond, name, other))

    def both(start_of):
        return start_of(core), start_of(1 - core)

    def far(t, name, src, dst, step, cond):
        def make():
            return pltpu.make_async_remote_copy(
                src_ref=view(t, src), dst_ref=view(t, dst),
                send_sem=far_send.at[t, step], recv_sem=recv_sem.at[t, index[name]],
                device_id=dev(x, y, z + step, core), device_id_type=pl.DeviceIdType.MESH,
            )

        @pl.when(cond)
        def _():
            make().start()

        finals.append((cond, make))

    true = z >= 0

    def own_load(t):
        hbm = (k_hbm, v_hbm)[t // CHUNKS].at[pl.ds((t % CHUNKS) * part, part), :]
        return pltpu.make_async_copy(hbm, view(t, at(0, col)), local_sem.at[t])

    def own(t):
        own_load(t).wait()
        for w, device, other in ways:
            send(t, ("M", w), at(0, col), at(0, col), device, other > col)
        for d in range(1, reach + 1):
            far(t, ("Z", d), at(0, col), at(d, col) if d < reach else extra(0), d, z + d < planes)
        for d in range(reach + 1, planes):
            far(t, "S", at(0, col), extra(1), d, (z == 0) & (col == 0))
        pair_copy(t, "own", at(0, col)).start()
        finals.append((true, lambda: pair_copy(t, "own", at(0, col))))
        pair_waits[t].append((true, "own", at(0, col, 1 - core)))

    def column(t, d):
        start_of = (lambda cc: at(d, col, cc)) if d < reach else (lambda cc: extra(0, cc))
        here, other = both(start_of)
        arrive(t, ("Z", d), here, other, z >= d)
        for w, device, j in ways:
            if d < reach:
                send(t, ("F", d, w), here, here, device, z >= d)
            else:
                send(t, ("M", w), here, at(0, col), device, (z >= d) & (j < col))
                send(t, "S", here, extra(1), device, (z == d) & (col == 0), w)

    def column_sink(t):
        arrive(t, "S", *both(lambda cc: extra(1, cc)), (z > reach) & (col == 0))
        for w, device, j in ways:
            send(t, "S", extra(1), extra(1), device, (z > reach) & (col == 0), w)

    def mixed(t, late):
        for w, device, j in ways:
            cond = ((j > col) & (z >= reach)) if late else (j < col)
            arrive(t, ("M", w), *both(lambda cc, j=j: at(0, j, cc)), cond)

    def full(t, d):
        for w, device, j in ways:
            arrive(t, ("F", d, w), *both(lambda cc, j=j: at(d, j, cc)), z >= d)

    def sink(t):
        arrive(t, "S", *both(lambda cc: extra(1, cc)), (z >= reach) & (col > 0))

    def from_pair(t):
        for cond, name, other in pair_waits[t]:
            @pl.when(cond)
            def _():
                pair_copy(t, name, other).wait_recv()

    for t in range(2 * CHUNKS):
        own_load(t).start()
    q_copy = pltpu.make_async_copy(q_hbm, qbuf, local_sem.at[2 * CHUNKS])
    q_copy.start()
    lens_copy = pltpu.make_async_copy(lens_hbm, lens_ref, local_sem.at[2 * CHUNKS + 1])
    lens_copy.start()
    barrier = pltpu.get_barrier_semaphore()
    for device in (to_x, to_y, to_d, partner):
        pl.semaphore_signal(barrier, inc=1, device_id=device, device_id_type=pl.DeviceIdType.MESH)
    for step in range(1, planes):
        pl.semaphore_signal(
            barrier, inc=1, device_id=dev(x, y, (z + step) % planes, core),
            device_id_type=pl.DeviceIdType.MESH,
        )
    pl.semaphore_wait(barrier, planes + 3)

    for t in range(2 * CHUNKS):
        own(t)

    def clear(start, count, cond):
        @pl.when(cond)
        def _():
            for buf in bufs:
                buf[start:start + count, :] = jnp.zeros((count, buf.shape[1]), buf.dtype)

    for d in range(1, reach):
        clear(d * plane, plane, z < d)
    for j in range(1, 4):
        clear(j * chip, chip, (j > col) & (z < reach))
    clear(reach * plane, 2 * chip, z < reach)

    q_pos = ctx * (4 * rows) + kvh * rows + lax.broadcasted_iota(jnp.int32, (rows, 1), 0)
    first = jnp.zeros((rows, 1), jnp.int32)
    begin = jnp.int32(0)
    lens_copy.wait()
    for n in range(lens_ref.shape[0]):
        first = jnp.where(q_pos >= begin, begin, first)
        begin = begin + lens_ref[n]
    lane = lax.broadcasted_iota(jnp.int32, (1, chip), 1)

    def set_bias(start, base):
        k_pos = base + lane
        sees = (k_pos <= q_pos) & ((k_pos >= first) | ((k_pos < SINK) & (k_pos >= 0)))
        bias[:, start:start + chip] = jnp.where(sees, jnp.float32(0.0), jnp.float32(NEG))

    nowhere = -planes * plane * 2
    for j in range(4):
        set_bias(j * chip, jnp.where(j <= col, z, z - reach) * plane + j * chip)
        for d in range(1, reach):
            set_bias(d * plane + j * chip, (z - d) * plane + j * chip)
    set_bias(reach * plane, (z - reach) * plane + col * chip)
    set_bias(reach * plane + chip, jnp.where((z > reach) | ((z == reach) & (col > 0)), 0, nowhere))

    first_half, second_half = range(CHUNKS), range(CHUNKS, 2 * CHUNKS)

    def columns(ts):
        for d in range(1, reach + 1):
            for t in ts:
                column(t, d)
        for t in ts:
            column_sink(t)

    def early(ts):
        for t in ts:
            mixed(t, False)
        for d in range(1, reach):
            for t in ts:
                full(t, d)

    def final(ts):
        for t in ts:
            sink(t)
            mixed(t, True)
        for t in ts:
            from_pair(t)

    columns(first_half)
    columns(second_half)
    early(first_half)
    early(second_half)
    final(first_half)
    q_copy.wait()

    keys = bias.shape[1]
    step = 2 * chip
    tall = group * rows
    size = HEAD_SIZE

    def head_q(h):
        return jnp.concatenate(
            [qbuf[:, (h * group + g) * size:(h * group + g + 1) * size] for g in range(group)], axis=0
        )

    def fold(op, value, total):
        for n in range(value.shape[1] // size):
            total = op(total, value[:, n * size:(n + 1) * size])
        return total

    def each(body, init):
        count = keys // step
        if count <= 8:
            for n in range(count):
                init = body(n, init)
            return init
        return lax.fori_loop(0, count, body, init)

    def cut(n):
        return pl.ds(n * step if isinstance(n, int) else pl.multiple_of(n * step, step), step)

    tops = []
    for h in range(kv_heads):
        qh = head_q(h)

        def score(n, top, h=h, qh=qh):
            s = lax.dot_general(
                qh, kbuf[cut(n), h * size:(h + 1) * size], (((1,), (1,)), ((), ())),
                preferred_element_type=jnp.float32,
            )
            s = s + jnp.concatenate([bias[:, cut(n)]] * group, axis=0)
            scores[h * tall:(h + 1) * tall, cut(n)] = s
            return fold(jnp.maximum, s, top)

        top = each(score, jnp.full((tall, size), NEG, jnp.float32))
        tops.append(jnp.max(top, axis=1, keepdims=True))

    final(second_half)

    factor = jnp.float32(HEAD_SIZE ** -0.5 * math.log2(math.e))
    for h in range(kv_heads):
        def weigh(n, carry, h=h):
            total, acc = carry
            p = jnp.exp2((scores[h * tall:(h + 1) * tall, cut(n)] - tops[h]) * factor)
            acc = acc + jnp.dot(
                p.astype(jnp.bfloat16), vbuf[cut(n), h * size:(h + 1) * size],
                preferred_element_type=jnp.float32,
            )
            return fold(jnp.add, p, total), acc

        zero = jnp.zeros((tall, size), jnp.float32)
        total, acc = each(weigh, (zero, zero))
        out = (acc / jnp.sum(total, axis=1, keepdims=True)).astype(o_ref.dtype)
        for g in range(group):
            o_ref[:, (h * group + g) * size:(h * group + g + 1) * size] = out[g * rows:(g + 1) * rows]

    for cond, make in finals:
        @pl.when(cond)
        def _():
            make().wait_send()


def solution(mesh):
    planes = mesh.shape["ctx"] // 2
    reach = planes // 2

    def shards(queries, keys, values, doc_lengths):
        rows, width = keys.shape
        kv_heads = width // HEAD_SIZE
        group = queries.shape[1] // width
        span = (4 * reach + 2) * 2 * rows
        room = span * (4 * width + 4 * (kv_heads * group + 1) * rows) + 8 * queries.size
        pieces = 2 + reach + 3 * (reach - 1) + 3
        return pl.pallas_call(
            functools.partial(attention_kernel, planes, reach, kv_heads, group),
            out_shape=jax.ShapeDtypeStruct(queries.shape, queries.dtype),
            in_specs=[pl.BlockSpec(memory_space=pltpu.HBM)] * 4,
            out_specs=pl.BlockSpec(memory_space=pltpu.VMEM),
            scratch_shapes=[
                pltpu.SMEM(doc_lengths.shape, doc_lengths.dtype),
                pltpu.VMEM((span, width), keys.dtype),
                pltpu.VMEM((span, width), values.dtype),
                pltpu.VMEM(queries.shape, queries.dtype),
                pltpu.VMEM((kv_heads * group * rows, span), jnp.float32),
                pltpu.VMEM((rows, span), jnp.float32),
                pltpu.SemaphoreType.DMA((2 * CHUNKS + 2,)),
                pltpu.SemaphoreType.DMA((2 * CHUNKS, pieces + 3)),
                pltpu.SemaphoreType.DMA((2 * CHUNKS, pieces)),
                pltpu.SemaphoreType.DMA((2 * CHUNKS, pieces)),
                pltpu.SemaphoreType.DMA((2 * CHUNKS, pieces)),
                pltpu.SemaphoreType.DMA((2 * CHUNKS, planes)),
            ],
            compiler_params=pltpu.CompilerParams(
                collective_id=0, has_side_effects=True, vmem_limit_bytes=min(room + 3 * 1024 * 1024, 64 * 1024 * 1024 - 65536),
            ),
            name="attend",
        )(*[pltpu.with_memory_space_constraint(a, pltpu.HBM) for a in (doc_lengths, queries, keys, values)])

    placed = (P(("ctx", "kvh"), None), P(("ctx", "kvh"), None), P(("ctx", "kvh"), None), P())
    return jax.shard_map(
        shards, mesh=mesh, in_specs=placed, out_specs=P(("ctx", "kvh"), None), check_vma=False
    )
```

time: 30.8 us -> 24.8 us (0.81)
  the two profiles are of different devices: /device:TPU:16 before, /device:TPU:30 now
where the time goes in v2:
time: 24.8 us; the launch traced here: 24.6 us
  Pallas kernels  23.9 us (96%)
  local copies, waits for them, and re-layouts  0.71 us (3%)
    pallas_call x1, Pallas kernels, shards(): pl.pallas_call(functools.partial(attention_kernel, planes, reach, kv_head...  23.9 us
    unnamed x1, local copies, waits for them, and re-layouts  0.71 us

profile of v2, /device:TPU:30, one launch (start us, length us, event | category | flops | bytes accessed | tf_op | source)
XLA Modules:
  0.0 24.6 jit_solution(140181522157084619)
XLA Ops:
  0.0 23.9 %attend.1 = bf16[64,2048]{1,0:T(8,128)(2,1)S(1)} custom-call(s32[16]{0:T(128)} %lens_hbm.1, bf16[64,2048]{1,0:T(8,128)(2,1)} %q_hbm.1, bf16[64,512]{1,0:T(8,128)(2,1)} %k_hbm.1, bf16[64,512]{1,0:T(8,128)(2,1)} %v_hbm.1), custom_call_target="tpu_custom_call" | custom-call | tf_op jit(solution)/shard_map/attend/pallas_call | solution.py:330
  23.9 0.7 %copy.6 = bf16[64,2048]{1,0:T(8,128)(2,1)} copy(bf16[64,2048]{1,0:T(8,128)(2,1)S(1)} %attend.1) | data formatting | bytes 524288
